TPU v7x, 32 devices: a whole 2x2x4 slice. The times are simulated.
32 devices in a mesh: dp: 4 (over x, core), expert: 8 (over z, y).
Axes of the slice: x: 2, y: 2, z: 4, core: 2. Of those that a mesh axis runs over, the one named last changes fastest.
Arguments:
- tokens: bfloat16 [128, 256, 1280], P(('dp', 'expert')), may hold values from -32 to 32
- slot_keys: bfloat16 [1280, 8], replicated, may hold values from -20 to 20
- logit_scale: float32 [1], replicated, may hold values from 8 to 16
- up_weight: bfloat16 [8, 1280, 5120], P('expert', None, 'dp'), may hold values from -0.15625 to 0.15625
- up_bias: bfloat16 [8, 5120], P('expert', 'dp'), may hold values from -3 to 3
- down_weight: bfloat16 [8, 5120, 1280], P('expert', 'dp'), may hold values from -0.078125 to 0.078125
- down_bias: bfloat16 [8, 1280], replicated, may hold values from -3 to 3
Outputs:
- mixed_out: bfloat16 [128, 256, 1280], P(('dp', 'expert'))
All inputs are finite; a program needn't handle non-finite values.
Results may differ from a plain program's by a relative error of at most 0.017.
Values may be sent and summed in bfloat16 or wider, within the bound.
No kernel may reach another device: no remote copies, remote signals or barrier semaphores. Data moves between devices by JAX's collectives and lax.ppermute only.
A program may use at most 64 MiB of HBM per device.

v0:
```python
import jax
import jax.numpy as jnp
from jax import lax
from jax.sharding import PartitionSpec as P

norm_eps = 1e-06


def unit_rms(values, axis_pos):
    return values * lax.rsqrt(jnp.mean(values * values, axis=axis_pos, keepdims=True) + norm_eps)


def body(tokens, slot_keys, logit_scale, up_weight, up_bias, down_weight, down_bias):
    images = tokens.shape[0]
    patches = tokens.shape[1]
    width = tokens.shape[2]
    per_owner = up_weight.shape[0]
    owners = lax.axis_size("expert")
    normed_tok = unit_rms(tokens.astype(jnp.float32), 2).astype(jnp.bfloat16)
    normed_keys = unit_rms(slot_keys.astype(jnp.float32), 0).astype(jnp.bfloat16)
    raw_scores = jnp.einsum(
        "ipd,dn->inp", normed_tok, normed_keys, preferred_element_type=jnp.float32
    )
    logits = logit_scale[0] * raw_scores / width
    dispatch = jax.nn.softmax(logits, axis=2).astype(jnp.bfloat16)
    combine = jax.nn.softmax(logits, axis=1).astype(jnp.bfloat16)
    slot_inputs = jnp.einsum(
        "inp,ipd->ind", dispatch, tokens, preferred_element_type=jnp.float32
    ).astype(jnp.bfloat16)
    routed = lax.all_to_all(slot_inputs, "expert", split_axis=1, concat_axis=0, tiled=True)
    pre = jnp.einsum(
        "rkd,kdf->rkf",
        lax.all_gather(routed, "dp", axis=0, tiled=True),
        up_weight,
        preferred_element_type=jnp.float32,
    )
    pre = pre + up_bias.astype(jnp.float32)[None]
    hidden = jax.nn.gelu(pre, approximate=False).astype(jnp.bfloat16)
    summed = lax.psum_scatter(
        jnp.einsum("rkf,kfd->rkd", hidden, down_weight, preferred_element_type=jnp.float32).astype(
            jnp.bfloat16
        ),
        "dp",
        scatter_dimension=0,
        tiled=True,
    ).astype(jnp.float32)
    own_bias = lax.dynamic_slice_in_dim(
        down_bias, lax.axis_index("expert") * per_owner, per_owner, 0
    ).astype(jnp.float32)
    finished = (
        (summed + own_bias[None]).astype(jnp.bfloat16).reshape(owners, images, per_owner, width)
    )
    returned = lax.all_to_all(finished, "expert", split_axis=0, concat_axis=0, tiled=True)
    weights = combine.reshape(images, owners, per_owner, patches)
    mixed_out = jnp.einsum("iekp,eikd->ipd", weights, returned, preferred_element_type=jnp.float32)
    return mixed_out.astype(jnp.bfloat16)


def solution(mesh):
    return jax.shard_map(
        body,
        mesh=mesh,
        in_specs=(
            P(("dp", "expert"), None, None),
            P(),
            P(),
            P("expert", None, "dp"),
            P("expert", "dp"),
            P("expert", "dp", None),
            P(),
        ),
        out_specs=P(("dp", "expert"), None, None),
        check_vma=False,
    )
```

profile of v0, /device:TPU:0, one launch (start us, length us, event | category | flops | bytes accessed | tf_op | source)
XLA Modules:
  0.0 83.9 jit_solution(10107239753829949492)
XLA Ops:
  6.5 0.0 copy-start
  7.3 1.0 %fusion.96 = f32[8]{0:T(128)S(1)} fusion(bf16[1280,8]{0,1:T(8,128)(2,1)} %param.8), kind=kLoop, calls=%fused_computation.87 | loop fusion | flops 30712 | bytes 20512 | tf_op jit(solution)/shard_map/reduce_sum | solution.py:10
  8.4 2.3 %fusion.2 = f32[4,256]{1,0:T(4,128)S(1)} fusion(bf16[4,256,1280]{2,1,0:T(8,128)(2,1)} %param.7), kind=kLoop, calls=%fused_computation.4 | loop fusion | flops 3931136 | bytes 2625536 | tf_op jit(solution)/shard_map/reduce_sum | solution.py:10
  10.7 0.0 copy-start.1
  10.7 2.6 %fusion.33 = f32[4,8,256]{2,1,0:T(8,128)S(1)} fusion(bf16[4,256,1280]{2,1,0:T(8,128)(2,1)} %param.7, f32[4,256]{1,0:T(4,128)S(1)} %add_rsqrt_fusion, bf16[1280,8]{0,1:T(8,128)(2,1)} %param.8, f32[8]{0:T(128)S(1)} %add_rsqrt_fusion.1, f32[]{:T(128)} %bitcast.139), kind=kOutput, calls=%fused_computation.24 | convolution fusion | flops 24950784 | bytes 2678820 | tf_op jit(solution)/shard_map/ipd,dn->inp/dot_general | solution.py:21
  13.3 0.2 fusion.133
  13.5 2.2 %convolution_convert_fusion.1 = bf16[4,8,1280]{2,1,0:T(8,128)(2,1)S(1)} fusion(bf16[4,256,1280]{2,1,0:T(8,128)(2,1)} %param.7, f32[4,8]{1,0:T(4,128)S(1)} %fusion.133, f32[4,8,256]{2,1,0:T(8,128)S(1)} %fusion.33), kind=kOutput, calls=%fused_computation.17 | convolution fusion | flops 21037344 | bytes 2736256 | tf_op jit(solution)/shard_map/inp,ipd->ind/dot_general | solution.py:27
  15.8 0.7 copy.11
  16.4 7.3 %all-to-all-start = ((bf16[4,8,1280]{2,0,1:T(4,128)(2,1)}), bf16[4,8,1280]{2,0,1:T(4,128)(2,1)S(1)}, u32[]{:S(2)}, u32[]{:S(2)}) async-start(bf16[4,8,1280]{2,0,1:T(4,128)(2,1)} %copy.11), calls=%async_computation | async-start | bytes 163840 | tf_op jit(solution)/shard_map/all_to_all | solution.py:30
  23.7 0.0 reduce-scatter.2.cloned.1.call-start
  23.8 0.0 copy-done.1
  23.8 6.9 %all-to-all-done = bf16[4,8,1280]{2,0,1:T(4,128)(2,1)S(1)} async-done(((bf16[4,8,1280]{2,0,1:T(4,128)(2,1)}), bf16[4,8,1280]{2,0,1:T(4,128)(2,1)S(1)}, u32[]{:S(2)}, u32[]{:S(2)}) %all-to-all-start) | async-done | bytes 81952 | tf_op jit(solution)/shard_map/all_to_all | solution.py:30
  30.8 6.6 %all_gather.3 = bf16[128,1,1280]{2,0,1:T(8,128)(2,1)} all-gather(bf16[32,1,1280]{2,0,1:T(8,128)(2,1)S(1)} %all_to_all.19), channel_id=1, replica_groups=mesh['dp'=4,'expert'=8] {'dp'}, dimensions={0}, use_global_device_ids=true | all-gather | bytes 409600 | tf_op jit(solution)/shard_map/all_gather | solution.py:33
  37.3 0.0 copy-done
  37.3 5.2 %fusion.20 = bf16[128,1,1280]{2,0,1:T(8,128)(2,1)} fusion(bf16[1,1280,1280]{2,1,0:T(8,128)(2,1)S(1)} %copy-done, bf16[1,1280,1280]{2,1,0:T(8,128)(2,1)} %param.10, bf16[128,1,1280]{2,0,1:T(8,128)(2,1)} %all_gather.3, f32[1280]{0:T(1024)S(1)} %convert_reduce_fusion.1), kind=kOutput, calls=%fused_computation.16 | convolution fusion | flops 849838080 | bytes 7214080 | tf_op jit(solution)/shard_map/rkf,kfd->rkd/dot_general | solution.py:40
  42.6 0.0 reduce-scatter.2.cloned.1.call-update
  42.6 0.8 convert_reduce_fusion
  43.3 17.3 %reduce-scatter.2.cloned.1.call-done = bf16[32,1,1280]{2,0,1:T(8,128)(2,1)} async-done(((bf16[128,1,1280]{2,0,1:T(8,128)(2,1)}), bf16[32,1,1280]{2,0,1:T(8,128)(2,1)}) %reduce-scatter.2.cloned.1.call-update) | async-done | bytes 81936 | tf_op jit(solution)/shard_map/reduce_scatter | solution.py:39
  60.6 0.9 %add_convert_fusion = bf16[32,1,1280]{2,0,1:T(8,128)(2,1)S(1)} fusion(bf16[32,1,1280]{2,0,1:T(8,128)(2,1)} %reduce-scatter.2.cloned.1.call-done, f32[1280]{0:T(1024)S(1)} %convert_reduce_fusion), kind=kLoop, calls=%fused_computation.82 | loop fusion | flops 122880 | bytes 168960 | tf_op jit(solution)/shard_map/convert_element_type | solution.py:51
  61.5 0.7 reshape.56
  62.2 5.5 %all-to-all-start.1 = ((bf16[8,4,1,1280]{3,1,2,0:T(4,128)(2,1)}), bf16[8,4,1,1280]{3,1,2,0:T(4,128)(2,1)S(1)}, u32[]{:S(2)}, u32[]{:S(2)}) async-start(bf16[8,4,1,1280]{3,1,2,0:T(4,128)(2,1)} %bitcast.16), calls=%async_computation.2 | async-start | bytes 163840 | tf_op jit(solution)/shard_map/all_to_all | solution.py:53
  67.7 7.0 %all-to-all-done.1 = bf16[8,4,1,1280]{3,1,2,0:T(4,128)(2,1)S(1)} async-done(((bf16[8,4,1,1280]{3,1,2,0:T(4,128)(2,1)}), bf16[8,4,1,1280]{3,1,2,0:T(4,128)(2,1)S(1)}, u32[]{:S(2)}, u32[]{:S(2)}) %all-to-all-start.1) | async-done | bytes 81952 | tf_op jit(solution)/shard_map/all_to_all | solution.py:53
  74.7 2.4 %convolution_convert_fusion = bf16[4,256,1280]{2,1,0:T(8,128)(2,1)} fusion(bf16[8,4,1,1280]{3,1,2,0:T(4,128)(2,1)S(1)} %all-to-all-done.1, f32[4,256]{1,0:T(4,128)S(1)} %fusion.134, f32[4,8,256]{2,1,0:T(8,128)S(1)} %fusion.33), kind=kOutput, calls=%fused_computation.6 | convolution fusion | flops 22307848 | bytes 2740224 | tf_op jit(solution)/shard_map/iekp,eikd->ipd/dot_general | solution.py:55
  (5 shorter events, 0.1 us)
Async XLA Ops:
  6.5 30.8 %copy-start = (bf16[1,1280,1280]{2,1,0:T(8,128)(2,1)S(1)}, bf16[1,1280,1280]{2,1,0:T(8,128)(2,1)}, u32[]{:S(2)}) copy-start(bf16[1,1280,1280]{2,1,0:T(8,128)(2,1)} %param.12) | copy-start | bytes 9830404
  10.7 13.1 %copy-start.1 = (bf16[1,1280]{1,0:T(2,128)(2,1)S(1)}, bf16[1,1280]{1,0:T(2,128)(2,1)}, u32[]{:S(2)}) copy-start(bf16[1,1280]{1,0:T(2,128)(2,1)} %param.11) | copy-start | bytes 7684
  16.4 14.3 %all-to-all-start = ((bf16[4,8,1280]{2,0,1:T(4,128)(2,1)}), bf16[4,8,1280]{2,0,1:T(4,128)(2,1)S(1)}, u32[]{:S(2)}, u32[]{:S(2)}) async-start(bf16[4,8,1280]{2,0,1:T(4,128)(2,1)} %copy.11), calls=%async_computation | async-start | bytes 163840 | tf_op jit(solution)/shard_map/all_to_all | solution.py:30
  23.7 36.9 %reduce-scatter.2.cloned.1.call-start = ((), (), s32[]{:S(2)}) async-start(), calls=%async_computation.3 | async-start | bytes 409600 | tf_op jit(solution)/shard_map/reduce_scatter | solution.py:39
  62.2 12.5 %all-to-all-start.1 = ((bf16[8,4,1,1280]{3,1,2,0:T(4,128)(2,1)}), bf16[8,4,1,1280]{3,1,2,0:T(4,128)(2,1)S(1)}, u32[]{:S(2)}, u32[]{:S(2)}) async-start(bf16[8,4,1,1280]{3,1,2,0:T(4,128)(2,1)} %bitcast.16), calls=%async_computation.2 | async-start | bytes 163840 | tf_op jit(solution)/shard_map/all_to_all | solution.py:53
Sparse Core Ops, SparseCore 0:
  42.7 17.8 reduce-scatter.1
where the time goes:
time: 84.4 us; the launch traced here: 83.9 us
  waiting for transfers between devices  31.2 us (37%)
  between operations  14.2 us (17%)
  starting transfers between devices  12.8 us (15%)
  matrix products  12.5 us (15%)
  blocking collectives  6.55 us (8%)
  other arithmetic  5.26 us (6%)
  local copies, waits for them, and re-layouts  1.37 us (2%)
    reduce_scatter x1, waiting for transfers between devices, body(): lax.psum_scatter(jnp.einsum('rkf,kfd->rkd', hidden, down_weight, preferre...  17.3 us
    all_to_all x1, starting transfers between devices, body(): lax.all_to_all(slot_inputs, 'expert', split_axis=1, concat_axis=0, tiled=...  7.31 us
    all_to_all x1, waiting for transfers between devices, body(): lax.all_to_all(finished, 'expert', split_axis=0, concat_axis=0, tiled=True)  6.98 us
    all_to_all x1, waiting for transfers between devices, body(): lax.all_to_all(slot_inputs, 'expert', split_axis=1, concat_axis=0, tiled=...  6.93 us
    all_gather x1, blocking collectives, body(): lax.all_gather(routed, 'dp', axis=0, tiled=True)  6.55 us
    all_to_all x1, starting transfers between devices, body(): lax.all_to_all(finished, 'expert', split_axis=0, concat_axis=0, tiled=True)  5.5 us
    dot_general x1, matrix products, body(): jnp.einsum('rkf,kfd->rkd', hidden, down_weight, preferred_element_type=jn...  5.22 us
    reduce_sum x2, other arithmetic, unit_rms(): jnp.mean(values * values, axis=axis_pos, keepdims=True) + norm_eps  3.35 us
  transfers between devices with their start and end apart: 3, of which 3 were waited for; matrix products, arithmetic and copies ran while one was open for 1% of the time, Pallas kernels for 0%

commit v1 on v0

--- a/solution.py
+++ b/solution.py
@@ -27,30 +27,36 @@
     slot_inputs = jnp.einsum(
         "inp,ipd->ind", dispatch, tokens, preferred_element_type=jnp.float32
     ).astype(jnp.bfloat16)
-    routed = lax.all_to_all(slot_inputs, "expert", split_axis=1, concat_axis=0, tiled=True)
+    replicas = lax.axis_size("dp")
+    everyone = ("dp", "expert")
+    outgoing = jnp.transpose(slot_inputs.reshape(images, owners, per_owner, width), (1, 0, 2, 3))
+    outgoing = jnp.broadcast_to(outgoing[None], (replicas,) + outgoing.shape).reshape(
+        replicas * owners, images, per_owner, width
+    )
+    gathered = lax.all_to_all(outgoing, everyone, split_axis=0, concat_axis=0, tiled=True)
     pre = jnp.einsum(
         "rkd,kdf->rkf",
-        lax.all_gather(routed, "dp", axis=0, tiled=True),
+        gathered.reshape(replicas * owners * images, per_owner, width),
         up_weight,
         preferred_element_type=jnp.float32,
     )
     pre = pre + up_bias.astype(jnp.float32)[None]
     hidden = jax.nn.gelu(pre, approximate=False).astype(jnp.bfloat16)
-    summed = lax.psum_scatter(
-        jnp.einsum("rkf,kfd->rkd", hidden, down_weight, preferred_element_type=jnp.float32).astype(
-            jnp.bfloat16
-        ),
-        "dp",
-        scatter_dimension=0,
+    partial = jnp.einsum(
+        "rkf,kfd->rkd", hidden, down_weight, preferred_element_type=jnp.float32
+    ).astype(jnp.bfloat16)
+    parts = lax.all_to_all(
+        partial.reshape(replicas * owners, images, per_owner, width),
+        everyone,
+        split_axis=0,
+        concat_axis=0,
         tiled=True,
-    ).astype(jnp.float32)
-    own_bias = lax.dynamic_slice_in_dim(
-        down_bias, lax.axis_index("expert") * per_owner, per_owner, 0
-    ).astype(jnp.float32)
-    finished = (
-        (summed + own_bias[None]).astype(jnp.bfloat16).reshape(owners, images, per_owner, width)
     )
-    returned = lax.all_to_all(finished, "expert", split_axis=0, concat_axis=0, tiled=True)
+    summed = jnp.sum(
+        parts.reshape(replicas, owners, images, per_owner, width).astype(jnp.float32), axis=0
+    )
+    bias = down_bias.astype(jnp.float32).reshape(owners, 1, per_owner, width)
+    returned = (summed + bias).astype(jnp.bfloat16)
     weights = combine.reshape(images, owners, per_owner, patches)
     mixed_out = jnp.einsum("iekp,eikd->ipd", weights, returned, preferred_element_type=jnp.float32)
     return mixed_out.astype(jnp.bfloat16)

time: 84.4 us -> 57.7 us (0.68)
  between operations: 14.2 us -> 0.88 us
  waiting for transfers between devices: 31.2 us -> 23.9 us
  blocking collectives: 6.55 us -> 0 us
  local copies, waits for them, and re-layouts: 1.37 us -> 4.42 us
  starting transfers between devices: 12.8 us -> 10.7 us
    reduce_scatter x1 -> x0, waiting for transfers between devices: 17.3 us -> none  [body(): lax.psum_scatter(jnp.einsum('rkf,kfd->rkd', hidden, down_weight, preferre...]
    all_to_all x2, waiting for transfers between devices: 13.9 us -> 23.9 us  [the longest x1 12 us: body(): lax.all_to_all(outgoing, everyone, split_axis=0, concat_axis=0, tiled=True)]
    all_gather x1 -> x0, blocking collectives: 6.55 us -> none  [body(): lax.all_gather(routed, 'dp', axis=0, tiled=True)]
    all_to_all x2, starting transfers between devices: 12.8 us -> 10.7 us  [the longest x1 7.44 us: body(): lax.all_to_all(outgoing, everyone, split_axis=0, concat_axis=0, tiled=True)]
    another operation x0 -> x1, local copies, waits for them, and re-layouts: none -> 1.77 us
    reduce_sum x0 -> x1, other arithmetic: none -> 1.17 us  [body(): jnp.sum(parts.reshape(replicas, owners, images, per_owner, width).astype(...]
    reshape x1, local copies, waits for them, and re-layouts: 0.66 us -> 1.78 us  [body(): partial.reshape(replicas * owners, images, per_owner, width)]
    broadcast_in_dim x0 -> x2, local copies, waits for them, and re-layouts: none -> 0.85 us  [body(): jnp.broadcast_to(outgoing[None], (replicas,) + outgoing.shape)]
  transfers between devices with their start and end apart: 3 -> 2, of which waited for: 3 -> 2; matrix products, arithmetic and copies ran while one was open for 1% -> 0% of each run, Pallas kernels for 0% -> 0%
where the time goes in v1:
time: 57.7 us; the launch traced here: 57.3 us
  waiting for transfers between devices  23.9 us (41%)
  matrix products  12.5 us (22%)
  starting transfers between devices  10.7 us (19%)
  other arithmetic  4.83 us (8%)
  local copies, waits for them, and re-layouts  4.42 us (8%)
  between operations  0.88 us (2%)
    all_to_all x1, waiting for transfers between devices, body(): lax.all_to_all(outgoing, everyone, split_axis=0, concat_axis=0, tiled=True)  12 us
    all_to_all x1, waiting for transfers between devices, body(): lax.all_to_all(partial.reshape(replicas * owners, images, per_owner, widt...  12 us
    all_to_all x1, starting transfers between devices, body(): lax.all_to_all(outgoing, everyone, split_axis=0, concat_axis=0, tiled=True)  7.44 us
    dot_general x1, matrix products, body(): jnp.einsum('rkf,kfd->rkd', hidden, down_weight, preferred_element_type=jn...  5.22 us
    reduce_sum x2, other arithmetic, unit_rms(): jnp.mean(values * values, axis=axis_pos, keepdims=True) + norm_eps  3.35 us
    all_to_all x1, starting transfers between devices, body(): lax.all_to_all(partial.reshape(replicas * owners, images, per_owner, widt...  3.3 us
    dot_general x1, matrix products, body(): jnp.einsum('ipd,dn->inp', normed_tok, normed_keys, preferred_element_type...  2.61 us
    dot_general x1, matrix products, body(): jnp.einsum('iekp,eikd->ipd', weights, returned, preferred_element_type=jn...  2.39 us
  transfers between devices with their start and end apart: 2, of which 2 were waited for; matrix products, arithmetic and copies ran while one was open for 0% of the time, Pallas kernels for 0%

profile of v1, /device:TPU:0, one launch (start us, length us, event | category | flops | bytes accessed | tf_op | source)
XLA Modules:
  0.0 57.3 jit_solution(1207821294639047478)
XLA Ops:
  0.0 0.0 copy-start
  0.8 1.0 %fusion.94 = f32[8]{0:T(128)S(1)} fusion(bf16[1280,8]{0,1:T(8,128)(2,1)} %param.8), kind=kLoop, calls=%fused_computation.87 | loop fusion | flops 30712 | bytes 20512 | tf_op jit(solution)/shard_map/reduce_sum | solution.py:10
  1.8 2.3 %fusion.2 = f32[4,256]{1,0:T(4,128)S(1)} fusion(bf16[4,256,1280]{2,1,0:T(8,128)(2,1)} %param.7), kind=kLoop, calls=%fused_computation.4 | loop fusion | flops 3931136 | bytes 2625536 | tf_op jit(solution)/shard_map/reduce_sum | solution.py:10
  4.2 0.0 copy-start.2
  4.2 2.6 %fusion.34 = f32[4,8,256]{2,1,0:T(8,128)S(1)} fusion(bf16[4,256,1280]{2,1,0:T(8,128)(2,1)} %param.7, f32[4,256]{1,0:T(4,128)S(1)} %add_rsqrt_fusion, bf16[1280,8]{0,1:T(8,128)(2,1)} %param.8, f32[8]{0:T(128)S(1)} %add_rsqrt_fusion.1, f32[]{:T(128)} %bitcast.139), kind=kOutput, calls=%fused_computation.25 | convolution fusion | flops 24950784 | bytes 2678820 | tf_op jit(solution)/shard_map/ipd,dn->inp/dot_general | solution.py:21
  6.8 0.2 fusion.131
  7.0 2.2 %fusion.23 = bf16[8,4,1280]{2,0,1:T(8,128)(2,1)S(1)} fusion(bf16[4,256,1280]{2,1,0:T(8,128)(2,1)} %param.7, f32[4,8]{1,0:T(4,128)S(1)} %fusion.131, f32[4,8,256]{2,1,0:T(8,128)S(1)} %fusion.34), kind=kOutput, calls=%fused_computation.18 | convolution fusion | flops 21037344 | bytes 2736256 | tf_op jit(solution)/shard_map/inp,ipd->ind/dot_general | solution.py:27
  9.3 0.8 %broadcast_in_dim.7 = bf16[4,8,4,1280]{3,2,1,0:T(4,128)(2,1)} broadcast(bf16[8,4,1280]{2,1,0:T(4,128)(2,1)S(1)} %copy.9), dimensions={1,2,3} | broadcast | bytes 409600 | tf_op jit(solution)/shard_map/broadcast_in_dim | solution.py:33
  10.1 7.4 %all-to-all-start = ((bf16[32,4,1,1280]{3,1,2,0:T(4,128)(2,1)}), bf16[32,4,1,1280]{3,1,2,0:T(4,128)(2,1)}, u32[]{:S(2)}, u32[]{:S(2)}) async-start(bf16[32,4,1,1280]{3,1,2,0:T(4,128)(2,1)} %bitcast.141), calls=%async_computation | async-start | bytes 655360 | tf_op jit(solution)/shard_map/all_to_all | solution.py:36
  17.5 0.0 copy-done.2
  17.6 12.0 %all-to-all-done = bf16[32,4,1,1280]{3,1,2,0:T(4,128)(2,1)} async-done(((bf16[32,4,1,1280]{3,1,2,0:T(4,128)(2,1)}), bf16[32,4,1,1280]{3,1,2,0:T(4,128)(2,1)}, u32[]{:S(2)}, u32[]{:S(2)}) %all-to-all-start) | async-done | bytes 327712 | tf_op jit(solution)/shard_map/all_to_all | solution.py:36
  29.5 1.8 %reshape.85 = bf16[128,1280]{1,0:T(8,128)(2,1)} reshape(bf16[32,4,1,1280]{3,1,2,0:T(4,128)(2,1)} %all-to-all-done) | data formatting | bytes 655360 | tf_op jit(solution)/shard_map/reshape.2
  31.3 0.0 copy-done
  31.3 0.0 copy-start.1
  31.3 5.2 %fusion.20 = bf16[128,1,1280]{2,0,1:T(8,128)(2,1)} fusion(bf16[1,1280,1280]{2,1,0:T(8,128)(2,1)S(1)} %copy-done, bf16[128,1280]{1,0:T(8,128)(2,1)} %reshape.85, bf16[1,1280,1280]{2,1,0:T(8,128)(2,1)} %param.10, f32[1280]{0:T(1024)S(1)} %convert_reduce_fusion.1), kind=kOutput, calls=%fused_computation.16 | convolution fusion | flops 849838080 | bytes 7214080 | tf_op jit(solution)/shard_map/rkf,kfd->rkd/dot_general | solution.py:45
  36.5 1.8 %reshape.89 = bf16[32,4,1,1280]{3,1,0,2:T(4,128)(2,1)} reshape(bf16[128,1,1280]{2,0,1:T(8,128)(2,1)} %fusion.20) | data formatting | bytes 655360 | tf_op jit(solution)/shard_map/reshape | solution.py:49
  38.3 3.3 %all-to-all-start.1 = ((bf16[32,4,1,1280]{3,1,2,0:T(4,128)(2,1)}), bf16[32,4,1,1280]{3,1,2,0:T(4,128)(2,1)}, u32[]{:S(2)}, u32[]{:S(2)}) async-start(bf16[32,4,1,1280]{3,1,2,0:T(4,128)(2,1)} %bitcast.140), calls=%async_computation.1 | async-start | bytes 655360 | tf_op jit(solution)/shard_map/all_to_all | solution.py:48
  41.6 0.0 copy-done.1
  41.7 12.0 %all-to-all-done.1 = bf16[32,4,1,1280]{3,1,2,0:T(4,128)(2,1)} async-done(((bf16[32,4,1,1280]{3,1,2,0:T(4,128)(2,1)}), bf16[32,4,1,1280]{3,1,2,0:T(4,128)(2,1)}, u32[]{:S(2)}, u32[]{:S(2)}) %all-to-all-start.1) | async-done | bytes 327712 | tf_op jit(solution)/shard_map/all_to_all | solution.py:48
  53.6 1.2 %convert_reduce_fusion = f32[8,4,1280]{2,1,0:T(4,128)S(1)} fusion(bf16[4,8,4,1280]{3,2,1,0:T(4,128)(2,1)} %bitcast.24), kind=kLoop, calls=%fused_computation.30 | loop fusion | flops 286720 | bytes 491520 | tf_op jit(solution)/shard_map/reduce_sum | solution.py:55
  54.9 2.4 %convolution_convert_fusion = bf16[4,256,1280]{2,1,0:T(8,128)(2,1)} fusion(bf16[8,4,1280]{2,1,0:T(4,128)(2,1)S(1)} %add_convert_fusion, f32[4,256]{1,0:T(4,128)S(1)} %fusion.132, f32[4,8,256]{2,1,0:T(8,128)S(1)} %fusion.34), kind=kOutput, calls=%fused_computation.6 | convolution fusion | flops 22307848 | bytes 2740224 | tf_op jit(solution)/shard_map/iekp,eikd->ipd/dot_general | solution.py:61
  (7 shorter events, 0.2 us)
Async XLA Ops:
  0.0 31.3 %copy-start = (bf16[1,1280,1280]{2,1,0:T(8,128)(2,1)S(1)}, bf16[1,1280,1280]{2,1,0:T(8,128)(2,1)}, u32[]{:S(2)}) copy-start(bf16[1,1280,1280]{2,1,0:T(8,128)(2,1)} %param.12) | copy-start | bytes 9830404
  4.2 13.4 %copy-start.2 = (bf16[1,1280]{1,0:T(2,128)(2,1)S(1)}, bf16[1,1280]{1,0:T(2,128)(2,1)}, u32[]{:S(2)}) copy-start(bf16[1,1280]{1,0:T(2,128)(2,1)} %param.11) | copy-start | bytes 7684
  10.1 19.5 %all-to-all-start = ((bf16[32,4,1,1280]{3,1,2,0:T(4,128)(2,1)}), bf16[32,4,1,1280]{3,1,2,0:T(4,128)(2,1)}, u32[]{:S(2)}, u32[]{:S(2)}) async-start(bf16[32,4,1,1280]{3,1,2,0:T(4,128)(2,1)} %bitcast.141), calls=%async_computation | async-start | bytes 655360 | tf_op jit(solution)/shard_map/all_to_all | solution.py:36
  31.3 10.3 %copy-start.1 = (bf16[8,1280]{1,0:T(8,128)(2,1)S(1)}, bf16[8,1280]{1,0:T(8,128)(2,1)}, u32[]{:S(2)}) copy-start(bf16[8,1280]{1,0:T(8,128)(2,1)} %param.13) | copy-start | bytes 61444
  38.3 15.3 %all-to-all-start.1 = ((bf16[32,4,1,1280]{3,1,2,0:T(4,128)(2,1)}), bf16[32,4,1,1280]{3,1,2,0:T(4,128)(2,1)}, u32[]{:S(2)}, u32[]{:S(2)}) async-start(bf16[32,4,1,1280]{3,1,2,0:T(4,128)(2,1)} %bitcast.140), calls=%async_computation.1 | async-start | bytes 655360 | tf_op jit(solution)/shard_map/all_to_all | solution.py:48

commit v2 on v1

v2 whole, which is shorter than its diff:
```python
import functools

import jax
import jax.numpy as jnp
from jax import lax
from jax.experimental import pallas as pl
from jax.experimental.pallas import tpu as pltpu
from jax.sharding import PartitionSpec as P

norm_eps = 1e-06
f32 = jnp.float32
bf16 = jnp.bfloat16
vmem = pl.BlockSpec(memory_space=pltpu.VMEM)
smem = pl.BlockSpec(memory_space=pltpu.SMEM)
hbm = pl.BlockSpec(memory_space=pl.ANY)


def front_kernel(replicas, scale_ref, keys_ref, tok_hbm, out_ref, comb_ref, tok, rows, sems):
    images, patches, width = tok.shape
    experts = keys_ref.shape[0]
    copies = [
        pltpu.make_async_copy(tok_hbm.at[i], tok.at[i], sems.at[i]) for i in range(images)
    ]
    for c in copies:
        c.start()
    keys = keys_ref[...].astype(f32)
    keys = keys * lax.rsqrt(jnp.mean(keys * keys, axis=1, keepdims=True) + norm_eps)
    keys = keys.astype(bf16)
    ones = jnp.ones((8, width), bf16)
    scale = scale_ref[0] / width
    nt = (((1,), (1,)), ((), ()))
    for i in range(images):
        copies[i].wait()
        x = tok[i]
        scores = lax.dot_general(keys, x, nt, preferred_element_type=f32)
        squares = lax.dot_general(ones, x * x, nt, preferred_element_type=f32)[0:1]
        logits = scores * (scale * lax.rsqrt(squares / width + norm_eps))
        over_tok = jnp.exp(logits - jnp.max(logits, axis=1, keepdims=True))
        dispatch = over_tok / jnp.sum(over_tok, axis=1, keepdims=True)
        over_slot = jnp.exp(logits - jnp.max(logits, axis=0, keepdims=True))
        comb_ref[i] = (over_slot / jnp.sum(over_slot, axis=0, keepdims=True)).astype(bf16)
        rows[:, i, :] = jnp.dot(dispatch.astype(bf16), x, preferred_element_type=f32)
    packed = rows[...].astype(bf16)
    for r in range(replicas):
        out_ref[r * experts : (r + 1) * experts] = packed


def front(replicas, scale, keys_t, tokens):
    images, patches, width = tokens.shape
    experts = keys_t.shape[0]
    return pl.pallas_call(
        functools.partial(front_kernel, replicas),
        in_specs=[smem, vmem, hbm],
        out_specs=[vmem, vmem],
        out_shape=[
            jax.ShapeDtypeStruct((replicas * experts, images, width), bf16),
            jax.ShapeDtypeStruct((images, experts, patches), bf16),
        ],
        scratch_shapes=[
            pltpu.VMEM((images, patches, width), bf16),
            pltpu.VMEM((experts, images, width), f32),
            pltpu.SemaphoreType.DMA((images,)),
        ],
        name="front",
    )(scale, keys_t, tokens)


def expert_kernel(x_ref, up_ref, up_bias_ref, down_ref, out_ref):
    senders, images, width = x_ref.shape
    x = x_ref[...].astype(f32).reshape(senders * images, width).astype(bf16)
    pre = jnp.dot(x, up_ref[0], preferred_element_type=f32)
    pre = pre + up_bias_ref[...].astype(f32)
    hidden = (0.5 * pre * (1.0 + lax.erf(pre * (0.5**0.5)))).astype(bf16)
    part = jnp.dot(hidden, down_ref[0], preferred_element_type=f32)
    out_ref[...] = part.reshape(senders, images, width).astype(bf16)


def expert(x, up, up_bias, down):
    return pl.pallas_call(
        expert_kernel,
        in_specs=[vmem] * 4,
        out_specs=vmem,
        out_shape=jax.ShapeDtypeStruct(x.shape, bf16),
        name="expert",
    )(x, up, up_bias, down)


def back_kernel(parts_ref, bias_ref, comb_ref, out_hbm, rows, out, sems):
    images, patches, width = out.shape
    experts = bias_ref.shape[0]
    replicas = parts_ref.shape[0] // experts
    total = parts_ref[0:experts].astype(f32)
    for r in range(1, replicas):
        total = total + parts_ref[r * experts : (r + 1) * experts].astype(f32)
    rows[...] = total
    bias = bias_ref[...].astype(f32)
    copies = []
    for i in range(images):
        y = (rows[:, i, :] + bias).astype(bf16)
        mixed = lax.dot_general(
            comb_ref[i], y, (((0,), (0,)), ((), ())), preferred_element_type=f32
        )
        out[i] = mixed.astype(bf16)
        copies.append(pltpu.make_async_copy(out.at[i], out_hbm.at[i], sems.at[i]))
        copies[i].start()
    for c in copies:
        c.wait()


def back(parts, bias, comb):
    images, experts, patches = comb.shape
    width = bias.shape[1]
    shape = (images, patches, width)
    return pl.pallas_call(
        back_kernel,
        in_specs=[vmem] * 3,
        out_specs=hbm,
        out_shape=jax.ShapeDtypeStruct(shape, bf16),
        scratch_shapes=[
            pltpu.VMEM((experts, images, width), f32),
            pltpu.VMEM(shape, bf16),
            pltpu.SemaphoreType.DMA((images,)),
        ],
        name="back",
    )(parts, bias, comb)


def body(tokens, slot_keys, logit_scale, up_weight, up_bias, down_weight, down_bias):
    replicas = lax.axis_size("dp")
    everyone = ("dp", "expert")
    outgoing, comb = front(replicas, logit_scale, slot_keys.T, tokens)
    gathered = lax.all_to_all(outgoing, everyone, split_axis=0, concat_axis=0, tiled=True)
    partial = expert(gathered, up_weight, up_bias, down_weight)
    parts = lax.all_to_all(partial, everyone, split_axis=0, concat_axis=0, tiled=True)
    return back(parts, down_bias, comb)


def solution(mesh):
    return jax.shard_map(
        body,
        mesh=mesh,
        in_specs=(
            P(("dp", "expert"), None, None),
            P(),
            P(),
            P("expert", None, "dp"),
            P("expert", "dp"),
            P("expert", "dp", None),
            P(),
        ),
        out_specs=P(("dp", "expert"), None, None),
        check_vma=False,
    )
```

time: 57.7 us -> 49.5 us (0.86)
  blocking collectives: 0 us -> 34.8 us
  waiting for transfers between devices: 23.9 us -> 0 us
  Pallas kernels: 0 us -> 13.7 us
  matrix products: 12.5 us -> 0 us
  starting transfers between devices: 10.7 us -> 0 us
  other arithmetic: 4.83 us -> 0 us
  local copies, waits for them, and re-layouts: 4.42 us -> 0 us
    all_to_all x0 -> x2, blocking collectives: none -> 34.8 us  [the longest x1 19.5 us: body(): lax.all_to_all(outgoing, everyone, split_axis=0, concat_axis=0, tiled=True)]
    all_to_all x2 -> x0, waiting for transfers between devices: 23.9 us -> none  [the longest x1 12 us: body(): lax.all_to_all(outgoing, everyone, split_axis=0, concat_axis=0, tiled=True)]
    pallas_call x0 -> x3, Pallas kernels: none -> 13.7 us  [the longest x1 5.88 us: front(): pl.pallas_call(functools.partial(front_kernel, replicas), in_specs=[smem,...]
    dot_general x4 -> x0, matrix products: 12.5 us -> none  [the longest x1 5.22 us: body(): jnp.einsum('rkf,kfd->rkd', hidden, down_weight, preferred_element_type=jn...]
    all_to_all x2 -> x0, starting transfers between devices: 10.7 us -> none  [the longest x1 7.44 us: body(): lax.all_to_all(outgoing, everyone, split_axis=0, concat_axis=0, tiled=True)]
    reduce_sum x3 -> x0, other arithmetic: 4.52 us -> none  [the longest x2 3.35 us: unit_rms(): jnp.mean(values * values, axis=axis_pos, keepdims=True) + norm_eps]
    reshape x1 -> x0, local copies, waits for them, and re-layouts: 1.78 us -> none  [body(): partial.reshape(replicas * owners, images, per_owner, width)]
    another operation x1 -> x0, local copies, waits for them, and re-layouts: 1.77 us -> none
  transfers between devices with their start and end apart: 2 -> 0, of which waited for: 2 -> 0; matrix products, arithmetic and copies ran while one was open for 0% -> 0% of each run, Pallas kernels for 0% -> 0%
where the time goes in v2:
time: 49.5 us; the launch traced here: 49.2 us
  blocking collectives  34.8 us (70%)
  Pallas kernels  13.7 us (28%)
  between operations  0.66 us (1%)
    all_to_all x1, blocking collectives, body(): lax.all_to_all(outgoing, everyone, split_axis=0, concat_axis=0, tiled=True)  19.5 us
    all_to_all x1, blocking collectives, body(): lax.all_to_all(partial, everyone, split_axis=0, concat_axis=0, tiled=True)  15.3 us
    pallas_call x1, Pallas kernels, front(): pl.pallas_call(functools.partial(front_kernel, replicas), in_specs=[smem,...  5.88 us
    pallas_call x1, Pallas kernels, expert(): pl.pallas_call(expert_kernel, in_specs=[vmem] * 4, out_specs=vmem, out_sh...  4.93 us
    pallas_call x1, Pallas kernels, back(): pl.pallas_call(back_kernel, in_specs=[vmem] * 3, out_specs=hbm, out_shape...  2.91 us

profile of v2, /device:TPU:0, one launch (start us, length us, event | category | flops | bytes accessed | tf_op | source)
XLA Modules:
  0.0 49.2 jit_solution(6034239936480878550)
XLA Ops:
  0.7 5.9 %front.1 = (bf16[32,4,1280]{2,1,0:T(4,128)(2,1)}, bf16[4,8,256]{2,1,0:T(8,128)(2,1)}) custom-call(f32[1]{0:T(128)S(6)} %copy.8.scale_ref, bf16[8,1280]{1,0:T(8,128)(2,1)} %bitcast.1, bf16[4,256,1280]{2,1,0:T(8,128)(2,1)} %tok_hbm.1), custom_call_target="tpu_custom_call" | custom-call | tf_op jit(solution)/shard_map/front/pallas_call | solution.py:51
  6.5 19.5 %all_to_all.10.x_ref = bf16[32,4,1280]{2,1,0:T(4,128)(2,1)} all-to-all(bf16[32,4,1280]{2,1,0:T(4,128)(2,1)} %get-tuple-element.7), channel_id=1, replica_groups=mesh['dp'=4,'expert'=8] {'dp','expert'}, dimensions={0} | all-to-all | bytes 655360 | tf_op jit(solution)/shard_map/all_to_all | solution.py:132
  26.0 4.9 %expert.1 = bf16[32,4,1280]{2,1,0:T(4,128)(2,1)} custom-call(bf16[32,4,1280]{2,1,0:T(4,128)(2,1)} %all_to_all.10.x_ref, bf16[1,1280,1280]{2,1,0:T(8,128)(2,1)} %up_ref.1, bf16[1,1280]{1,0:T(2,128)(2,1)} %up_bias_ref.1, bf16[1,1280,1280]{2,1,0:T(8,128)(2,1)} %down_ref.1), custom_call_target="tpu_custom_call" | custom-call | tf_op jit(solution)/shard_map/expert/pallas_call | solution.py:79
  30.9 15.3 %all_to_all.11.parts_ref = bf16[32,4,1280]{2,1,0:T(4,128)(2,1)} all-to-all(bf16[32,4,1280]{2,1,0:T(4,128)(2,1)} %expert.1), channel_id=1, replica_groups=mesh['dp'=4,'expert'=8] {'dp','expert'}, dimensions={0} | all-to-all | bytes 655360 | tf_op jit(solution)/shard_map/all_to_all | solution.py:134
  46.2 2.9 %back.1 = bf16[4,256,1280]{2,1,0:T(8,128)(2,1)} custom-call(bf16[32,4,1280]{2,1,0:T(4,128)(2,1)} %all_to_all.11.parts_ref, bf16[8,1280]{1,0:T(8,128)(2,1)} %bias_ref.1, bf16[4,8,256]{2,1,0:T(8,128)(2,1)} %get-tuple-element.8.comb_ref), custom_call_target="tpu_custom_call" | custom-call | tf_op jit(solution)/shard_map/back/pallas_call | solution.py:114

commit v3 on v2

--- a/solution.py
+++ b/solution.py
@@ -12,15 +12,18 @@
 bf16 = jnp.bfloat16
 vmem = pl.BlockSpec(memory_space=pltpu.VMEM)
 smem = pl.BlockSpec(memory_space=pltpu.SMEM)
-hbm = pl.BlockSpec(memory_space=pl.ANY)
+hbm = pl.BlockSpec(memory_space=pltpu.HBM)
 
 
-def front_kernel(replicas, scale_ref, keys_ref, tok_hbm, out_ref, comb_ref, tok, rows, sems):
+def front_kernel(
+    replicas, scale_ref, keys_ref, tok_hbm, down_hbm, out_ref, comb_ref, down_ref, tok, rows, sems
+):
     images, patches, width = tok.shape
     experts = keys_ref.shape[0]
     copies = [
         pltpu.make_async_copy(tok_hbm.at[i], tok.at[i], sems.at[i]) for i in range(images)
     ]
+    copies.append(pltpu.make_async_copy(down_hbm, down_ref, sems.at[images]))
     for c in copies:
         c.start()
     keys = keys_ref[...].astype(f32)
@@ -43,26 +46,34 @@
     packed = rows[...].astype(bf16)
     for r in range(replicas):
         out_ref[r * experts : (r + 1) * experts] = packed
+    copies[images].wait()
 
 
-def front(replicas, scale, keys_t, tokens):
+def front(replicas, scale, keys_t, tokens, down):
     images, patches, width = tokens.shape
     experts = keys_t.shape[0]
     return pl.pallas_call(
         functools.partial(front_kernel, replicas),
-        in_specs=[smem, vmem, hbm],
-        out_specs=[vmem, vmem],
+        in_specs=[smem, vmem, hbm, hbm],
+        out_specs=[vmem, vmem, vmem],
         out_shape=[
             jax.ShapeDtypeStruct((replicas * experts, images, width), bf16),
             jax.ShapeDtypeStruct((images, experts, patches), bf16),
+            pltpu.VMEM(down.shape, bf16),
         ],
         scratch_shapes=[
             pltpu.VMEM((images, patches, width), bf16),
             pltpu.VMEM((experts, images, width), f32),
-            pltpu.SemaphoreType.DMA((images,)),
+            pltpu.SemaphoreType.DMA((images + 1,)),
         ],
+        compiler_params=pltpu.CompilerParams(vmem_limit_bytes=12 << 20),
+        cost_estimate=pl.CostEstimate(
+            flops=4 * (experts + 8) * tokens.size,
+            transcendentals=2 * images * experts * patches,
+            bytes_accessed=8 * tokens.size,
+        ),
         name="front",
-    )(scale, keys_t, tokens)
+    )(scale, keys_t, tokens, down)
 
 
 def expert_kernel(x_ref, up_ref, up_bias_ref, down_ref, out_ref):
@@ -81,6 +92,7 @@
         in_specs=[vmem] * 4,
         out_specs=vmem,
         out_shape=jax.ShapeDtypeStruct(x.shape, bf16),
+        compiler_params=pltpu.CompilerParams(vmem_limit_bytes=16 << 20),
         name="expert",
     )(x, up, up_bias, down)
 
@@ -121,6 +133,7 @@
             pltpu.VMEM(shape, bf16),
             pltpu.SemaphoreType.DMA((images,)),
         ],
+        compiler_params=pltpu.CompilerParams(vmem_limit_bytes=12 << 20),
         name="back",
     )(parts, bias, comb)
 
@@ -128,9 +141,15 @@
 def body(tokens, slot_keys, logit_scale, up_weight, up_bias, down_weight, down_bias):
     replicas = lax.axis_size("dp")
     everyone = ("dp", "expert")
-    outgoing, comb = front(replicas, logit_scale, slot_keys.T, tokens)
+    outgoing, comb, down_near = front(
+        replicas,
+        logit_scale,
+        slot_keys.T,
+        pltpu.with_memory_space_constraint(tokens, pltpu.HBM),
+        pltpu.with_memory_space_constraint(down_weight, pltpu.HBM),
+    )
     gathered = lax.all_to_all(outgoing, everyone, split_axis=0, concat_axis=0, tiled=True)
-    partial = expert(gathered, up_weight, up_bias, down_weight)
+    partial = expert(gathered, up_weight, up_bias, down_near)
     parts = lax.all_to_all(partial, everyone, split_axis=0, concat_axis=0, tiled=True)
     return back(parts, down_bias, comb)
 

time: 49.5 us -> 42.6 us (0.86)
  Pallas kernels: 13.7 us -> 7.67 us
  blocking collectives: 34.8 us -> 33.3 us
  local copies, waits for them, and re-layouts: 0 us -> 0.73 us
    pallas_call x1, Pallas kernels: 4.93 us -> 1.16 us  [expert(): pl.pallas_call(expert_kernel, in_specs=[vmem] * 4, out_specs=vmem, out_sh...]
    pallas_call x1, Pallas kernels: 5.88 us -> 4.59 us  [front(): pl.pallas_call(functools.partial(front_kernel, replicas), in_specs=[smem,...]
    all_to_all x1, blocking collectives: 15.3 us -> 14.2 us  [body(): lax.all_to_all(partial, everyone, split_axis=0, concat_axis=0, tiled=True)]
    pallas_call x1, Pallas kernels: 2.91 us -> 1.91 us  [back(): pl.pallas_call(back_kernel, in_specs=[vmem] * 3, out_specs=hbm, out_shape...]
    unnamed x0 -> x8, local copies, waits for them, and re-layouts: none -> 0.73 us
where the time goes in v3:
time: 42.6 us; the launch traced here: 42.4 us
  blocking collectives  33.3 us (78%)
  Pallas kernels  7.67 us (18%)
  local copies, waits for them, and re-layouts  0.73 us (2%)
  between operations  0.68 us (2%)
    all_to_all x1, blocking collectives, body(): lax.all_to_all(outgoing, everyone, split_axis=0, concat_axis=0, tiled=True)  19.2 us
    all_to_all x1, blocking collectives, body(): lax.all_to_all(partial, everyone, split_axis=0, concat_axis=0, tiled=True)  14.2 us
    pallas_call x1, Pallas kernels, front(): pl.pallas_call(functools.partial(front_kernel, replicas), in_specs=[smem,...  4.59 us
    pallas_call x1, Pallas kernels, back(): pl.pallas_call(back_kernel, in_specs=[vmem] * 3, out_specs=hbm, out_shape...  1.91 us
    pallas_call x1, Pallas kernels, expert(): pl.pallas_call(expert_kernel, in_specs=[vmem] * 4, out_specs=vmem, out_sh...  1.16 us

profile of v3, /device:TPU:0, one launch (start us, length us, event | category | flops | bytes accessed | tf_op | source)
XLA Modules:
  0.0 42.4 jit_solution(2758088610172242394)
XLA Ops:
  0.7 0.0 copy-start.2
  0.7 0.7 %copy-done.2 = bf16[1280,8]{0,1:T(8,128)(2,1)S(1)} copy-done((bf16[1280,8]{0,1:T(8,128)(2,1)S(1)}, bf16[1280,8]{0,1:T(8,128)(2,1)}, u32[]{:S(2)}) %copy-start.2) | copy-done | bytes 20504
  1.4 0.0 copy-start
  1.4 0.0 copy-start.3
  1.4 4.6 %front.1 = (bf16[32,4,1280]{2,1,0:T(4,128)(2,1)S(1)}, bf16[4,8,256]{2,1,0:T(8,128)(2,1)S(1)}, bf16[1,1280,1280]{2,1,0:T(8,128)(2,1)S(1)}) custom-call(f32[1]{0:T(128)S(6)} %copy.8.scale_ref, bf16[8,1280]{1,0:T(8,128)(2,1)S(1)} %bitcast.1, bf16[4,256,1280]{2,1,0:T(8,128)(2,1)} %tok_hbm.1, bf16[1,1280,1280]{2,1,0:T(8,128)(2,1)} %down_hbm.1), custom_call_target="tpu_custom_call" | custom-call | flops 83886080 | bytes 10485760 | tf_op jit(solution)/shard_map/front/pallas_call | solution.py:55
  6.0 19.2 %all_to_all.10.x_ref = bf16[32,4,1280]{2,1,0:T(4,128)(2,1)S(1)} all-to-all(bf16[32,4,1280]{2,1,0:T(4,128)(2,1)S(1)} %get-tuple-element.8), channel_id=1, replica_groups=mesh['dp'=4,'expert'=8] {'dp','expert'}, dimensions={0} | all-to-all | bytes 655360 | tf_op jit(solution)/shard_map/all_to_all | solution.py:151
  25.1 0.0 copy-done
  25.1 0.0 copy-done.3
  25.1 0.0 copy-start.1
  25.1 1.2 %expert.1 = bf16[32,4,1280]{2,1,0:T(4,128)(2,1)S(1)} custom-call(bf16[32,4,1280]{2,1,0:T(4,128)(2,1)S(1)} %all_to_all.10.x_ref, bf16[1,1280,1280]{2,1,0:T(8,128)(2,1)S(1)} %copy-done, bf16[1,1280]{1,0:T(2,128)(2,1)S(1)} %copy-done.3, bf16[1,1280,1280]{2,1,0:T(8,128)(2,1)S(1)} %get-tuple-element.9.down_ref), custom_call_target="tpu_custom_call" | custom-call | tf_op jit(solution)/shard_map/expert/pallas_call | solution.py:90
  26.3 14.2 %all_to_all.11.parts_ref = bf16[32,4,1280]{2,1,0:T(4,128)(2,1)S(1)} all-to-all(bf16[32,4,1280]{2,1,0:T(4,128)(2,1)S(1)} %expert.1), channel_id=1, replica_groups=mesh['dp'=4,'expert'=8] {'dp','expert'}, dimensions={0} | all-to-all | bytes 655360 | tf_op jit(solution)/shard_map/all_to_all | solution.py:153
  40.5 0.0 copy-done.1
  40.5 1.9 %back.1 = bf16[4,256,1280]{2,1,0:T(8,128)(2,1)} custom-call(bf16[32,4,1280]{2,1,0:T(4,128)(2,1)S(1)} %all_to_all.11.parts_ref, bf16[8,1280]{1,0:T(8,128)(2,1)S(1)} %copy-done.1, bf16[4,8,256]{2,1,0:T(8,128)(2,1)S(1)} %get-tuple-element.10.comb_ref), custom_call_target="tpu_custom_call" | custom-call | tf_op jit(solution)/shard_map/back/pallas_call | solution.py:126
Async XLA Ops:
  0.7 0.7 %copy-start.2 = (bf16[1280,8]{0,1:T(8,128)(2,1)S(1)}, bf16[1280,8]{0,1:T(8,128)(2,1)}, u32[]{:S(2)}) copy-start(bf16[1280,8]{0,1:T(8,128)(2,1)} %param.8) | copy-start | bytes 61444
  1.4 23.8 %copy-start = (bf16[1,1280,1280]{2,1,0:T(8,128)(2,1)S(1)}, bf16[1,1280,1280]{2,1,0:T(8,128)(2,1)}, u32[]{:S(2)}) copy-start(bf16[1,1280,1280]{2,1,0:T(8,128)(2,1)} %up_ref.1) | copy-start | bytes 9830404
  1.4 23.8 %copy-start.3 = (bf16[1,1280]{1,0:T(2,128)(2,1)S(1)}, bf16[1,1280]{1,0:T(2,128)(2,1)}, u32[]{:S(2)}) copy-start(bf16[1,1280]{1,0:T(2,128)(2,1)} %up_bias_ref.1) | copy-start | bytes 7684
  25.1 15.4 %copy-start.1 = (bf16[8,1280]{1,0:T(8,128)(2,1)S(1)}, bf16[8,1280]{1,0:T(8,128)(2,1)}, u32[]{:S(2)}) copy-start(bf16[8,1280]{1,0:T(8,128)(2,1)} %bias_ref.1) | copy-start | bytes 61444

commit v4 on v3

--- a/solution.py
+++ b/solution.py
@@ -16,7 +16,18 @@
 
 
 def front_kernel(
-    replicas, scale_ref, keys_ref, tok_hbm, down_hbm, out_ref, comb_ref, down_ref, tok, rows, sems
+    replicas,
+    scale_ref,
+    keys_hbm,
+    tok_hbm,
+    down_hbm,
+    out_ref,
+    comb_ref,
+    down_ref,
+    keys_ref,
+    tok,
+    rows,
+    sems,
 ):
     images, patches, width = tok.shape
     experts = keys_ref.shape[0]
@@ -24,8 +35,13 @@
         pltpu.make_async_copy(tok_hbm.at[i], tok.at[i], sems.at[i]) for i in range(images)
     ]
     copies.append(pltpu.make_async_copy(down_hbm, down_ref, sems.at[images]))
-    for c in copies:
+    small = [
+        pltpu.make_async_copy(keys_hbm, keys_ref, sems.at[images + 1]),
+    ]
+    for c in small + copies:
         c.start()
+    for c in small:
+        c.wait()
     keys = keys_ref[...].astype(f32)
     keys = keys * lax.rsqrt(jnp.mean(keys * keys, axis=1, keepdims=True) + norm_eps)
     keys = keys.astype(bf16)
@@ -54,7 +70,7 @@
     experts = keys_t.shape[0]
     return pl.pallas_call(
         functools.partial(front_kernel, replicas),
-        in_specs=[smem, vmem, hbm, hbm],
+        in_specs=[smem, hbm, hbm, hbm],
         out_specs=[vmem, vmem, vmem],
         out_shape=[
             jax.ShapeDtypeStruct((replicas * experts, images, width), bf16),
@@ -62,9 +78,10 @@
             pltpu.VMEM(down.shape, bf16),
         ],
         scratch_shapes=[
+            pltpu.VMEM(keys_t.shape, bf16),
             pltpu.VMEM((images, patches, width), bf16),
             pltpu.VMEM((experts, images, width), f32),
-            pltpu.SemaphoreType.DMA((images + 1,)),
+            pltpu.SemaphoreType.DMA((images + 2,)),
         ],
         compiler_params=pltpu.CompilerParams(vmem_limit_bytes=12 << 20),
         cost_estimate=pl.CostEstimate(
@@ -144,7 +161,7 @@
     outgoing, comb, down_near = front(
         replicas,
         logit_scale,
-        slot_keys.T,
+        pltpu.with_memory_space_constraint(slot_keys.T, pltpu.HBM),
         pltpu.with_memory_space_constraint(tokens, pltpu.HBM),
         pltpu.with_memory_space_constraint(down_weight, pltpu.HBM),
     )

time: 42.6 us -> 41.9 us (0.984)
  local copies, waits for them, and re-layouts: 0.73 us -> 0.01 us
    unnamed x8 -> x6, local copies, waits for them, and re-layouts: 0.73 us -> 0.01 us
where the time goes in v4:
time: 41.9 us; the launch traced here: 41.7 us
  blocking collectives  33.3 us (79%)
  Pallas kernels  7.7 us (18%)
  between operations  0.69 us (2%)
    all_to_all x1, blocking collectives, body(): lax.all_to_all(outgoing, everyone, split_axis=0, concat_axis=0, tiled=True)  19.2 us
    all_to_all x1, blocking collectives, body(): lax.all_to_all(partial, everyone, split_axis=0, concat_axis=0, tiled=True)  14.2 us
    pallas_call x1, Pallas kernels, front(): pl.pallas_call(functools.partial(front_kernel, replicas), in_specs=[smem,...  4.62 us
    pallas_call x1, Pallas kernels, back(): pl.pallas_call(back_kernel, in_specs=[vmem] * 3, out_specs=hbm, out_shape...  1.91 us
    pallas_call x1, Pallas kernels, expert(): pl.pallas_call(expert_kernel, in_specs=[vmem] * 4, out_specs=vmem, out_sh...  1.16 us

profile of v4, /device:TPU:0, one launch (start us, length us, event | category | flops | bytes accessed | tf_op | source)
XLA Modules:
  0.0 41.7 jit_solution(8687298590282036076)
XLA Ops:
  0.7 0.0 copy-start
  0.7 0.0 copy-start.2
  0.7 4.6 %front.1 = (bf16[32,4,1280]{2,1,0:T(4,128)(2,1)S(1)}, bf16[4,8,256]{2,1,0:T(8,128)(2,1)S(1)}, bf16[1,1280,1280]{2,1,0:T(8,128)(2,1)S(1)}) custom-call(f32[1]{0:T(128)S(6)} %copy.8.scale_ref, bf16[8,1280]{1,0:T(8,128)(2,1)} %bitcast.1, bf16[4,256,1280]{2,1,0:T(8,128)(2,1)} %tok_hbm.1, bf16[1,1280,1280]{2,1,0:T(8,128)(2,1)} %down_hbm.1), custom_call_target="tpu_custom_call" | custom-call | flops 83886080 | bytes 10485760 | tf_op jit(solution)/shard_map/front/pallas_call | solution.py:71
  5.3 19.2 %all_to_all.10.x_ref = bf16[32,4,1280]{2,1,0:T(4,128)(2,1)S(1)} all-to-all(bf16[32,4,1280]{2,1,0:T(4,128)(2,1)S(1)} %get-tuple-element.8), channel_id=1, replica_groups=mesh['dp'=4,'expert'=8] {'dp','expert'}, dimensions={0} | all-to-all | bytes 655360 | tf_op jit(solution)/shard_map/all_to_all | solution.py:168
  24.5 0.0 copy-done
  24.5 0.0 copy-done.2
  24.5 0.0 copy-start.1
  24.5 1.2 %expert.1 = bf16[32,4,1280]{2,1,0:T(4,128)(2,1)S(1)} custom-call(bf16[32,4,1280]{2,1,0:T(4,128)(2,1)S(1)} %all_to_all.10.x_ref, bf16[1,1280,1280]{2,1,0:T(8,128)(2,1)S(1)} %copy-done, bf16[1,1280]{1,0:T(2,128)(2,1)S(1)} %copy-done.2, bf16[1,1280,1280]{2,1,0:T(8,128)(2,1)S(1)} %get-tuple-element.9.down_ref), custom_call_target="tpu_custom_call" | custom-call | tf_op jit(solution)/shard_map/expert/pallas_call | solution.py:107
  25.6 14.2 %all_to_all.11.parts_ref = bf16[32,4,1280]{2,1,0:T(4,128)(2,1)S(1)} all-to-all(bf16[32,4,1280]{2,1,0:T(4,128)(2,1)S(1)} %expert.1), channel_id=1, replica_groups=mesh['dp'=4,'expert'=8] {'dp','expert'}, dimensions={0} | all-to-all | bytes 655360 | tf_op jit(solution)/shard_map/all_to_all | solution.py:170
  39.8 0.0 copy-done.1
  39.8 1.9 %back.1 = bf16[4,256,1280]{2,1,0:T(8,128)(2,1)} custom-call(bf16[32,4,1280]{2,1,0:T(4,128)(2,1)S(1)} %all_to_all.11.parts_ref, bf16[8,1280]{1,0:T(8,128)(2,1)S(1)} %copy-done.1, bf16[4,8,256]{2,1,0:T(8,128)(2,1)S(1)} %get-tuple-element.10.comb_ref), custom_call_target="tpu_custom_call" | custom-call | tf_op jit(solution)/shard_map/back/pallas_call | solution.py:143
Async XLA Ops:
  0.7 23.8 %copy-start = (bf16[1,1280,1280]{2,1,0:T(8,128)(2,1)S(1)}, bf16[1,1280,1280]{2,1,0:T(8,128)(2,1)}, u32[]{:S(2)}) copy-start(bf16[1,1280,1280]{2,1,0:T(8,128)(2,1)} %up_ref.1) | copy-start | bytes 9830404
  0.7 23.8 %copy-start.2 = (bf16[1,1280]{1,0:T(2,128)(2,1)S(1)}, bf16[1,1280]{1,0:T(2,128)(2,1)}, u32[]{:S(2)}) copy-start(bf16[1,1280]{1,0:T(2,128)(2,1)} %up_bias_ref.1) | copy-start | bytes 7684
  24.5 15.4 %copy-start.1 = (bf16[8,1280]{1,0:T(8,128)(2,1)S(1)}, bf16[8,1280]{1,0:T(8,128)(2,1)}, u32[]{:S(2)}) copy-start(bf16[8,1280]{1,0:T(8,128)(2,1)} %bias_ref.1) | copy-start | bytes 61444
